TPU v7x, 32 devices: a whole 2x2x4 slice. The times are simulated.
32 devices in a mesh: ta: 4 (over z), gz: 2 (over x), gy: 4 (over y, core).
Axes of the slice: x: 2, y: 2, z: 4, core: 2. Of those that a mesh axis runs over, the one named last changes fastest.
Arguments:
- lattice_links: float32 [2, 4, 18, 8, 16, 1024], P(None, None, None, 'ta', 'gz', 'gy'), may hold values from -1 to 1, as said below
- transform: float32 [2, 18, 8, 16, 1024], P(None, None, 'ta', 'gz', 'gy'), may hold values from -1 to 1, as said below
Outputs:
- fixed_transform: float32 [2, 18, 8, 16, 1024], P(None, None, 'ta', 'gz', 'gy')
- monitor: float32 [2, 2], replicated
Inputs may be any that keep to these rules, and one draw needn't show every extreme that they name: `lattice_links`: every site's matrix for every colour and direction is special unitary. `transform`: every site's matrix is special unitary.
All inputs are finite; a program needn't handle non-finite values.
Results may differ from a plain program's by a relative error of at most 0.0003.
Values sent between devices are 32-bit elements; how exact they have to be, the bound alone decides.
A program may use at most 128 MiB of HBM per device.

v0:
```python
import functools

import jax
import jax.numpy as jnp
from jax import lax
from jax.experimental import pallas as pl
from jax.experimental.pallas import tpu as pltpu
from jax.sharding import PartitionSpec as P

NX = 64
ITERS = 2
OMEGA = 1.7
GUARD = 1e-12
LANES = 128
AXES = ("ta", "gz", "gy")
MESH = pl.DeviceIdType.MESH


def total(terms):
    out = terms[0]
    for term in terms[1:]:
        out = out + term
    return out


def mul(a, b):
    re, im = [], []
    for i in range(3):
        for j in range(3):
            re.append(
                total([a[3 * i + k] * b[3 * k + j] for k in range(3)])
                - total([a[9 + 3 * i + k] * b[9 + 3 * k + j] for k in range(3)])
            )
            im.append(
                total([a[3 * i + k] * b[9 + 3 * k + j] for k in range(3)])
                + total([a[9 + 3 * i + k] * b[3 * k + j] for k in range(3)])
            )
    return re + im


def mul_adj(a, b):
    re, im = [], []
    for i in range(3):
        for j in range(3):
            re.append(
                total([a[3 * i + k] * b[3 * j + k] for k in range(3)])
                + total([a[9 + 3 * i + k] * b[9 + 3 * j + k] for k in range(3)])
            )
            im.append(
                total([a[9 + 3 * i + k] * b[3 * j + k] for k in range(3)])
                - total([a[3 * i + k] * b[9 + 3 * j + k] for k in range(3)])
            )
    return re + im


def add(a, b):
    return [x + y for x, y in zip(a, b)]


def add_adj(a, b):
    out = []
    for i in range(3):
        for j in range(3):
            out.append(a[3 * i + j] + b[3 * j + i])
    for i in range(3):
        for j in range(3):
            out.append(a[9 + 3 * i + j] - b[9 + 3 * j + i])
    return out


def rotation(a, i, j):
    ii, jj, ij, ji = 4 * i, 4 * j, 3 * i + j, 3 * j + i
    v0 = a[ii] + a[jj]
    v1 = -(a[9 + ij] + a[9 + ji])
    v2 = a[ji] - a[ij]
    v3 = a[9 + jj] - a[9 + ii]
    tail = v1 * v1 + v2 * v2 + v3 * v3
    length = jnp.sqrt(v0 * v0 + tail)
    s0 = (1.0 - OMEGA) * length + OMEGA * v0
    inv = lax.rsqrt(s0 * s0 + (OMEGA * OMEGA) * tail + GUARD)
    scaled = OMEGA * inv
    return (s0 * inv, v1 * scaled, v2 * scaled, v3 * scaled)


def rotate(m, q, i, j):
    q0, q1, q2, q3 = q
    out = list(m)
    for k in range(3):
        ur, ui = m[3 * i + k], m[9 + 3 * i + k]
        lr, li = m[3 * j + k], m[9 + 3 * j + k]
        out[3 * i + k] = q0 * ur - q3 * ui + q2 * lr - q1 * li
        out[9 + 3 * i + k] = q0 * ui + q3 * ur + q2 * li + q1 * lr
        out[3 * j + k] = q0 * lr + q3 * li - q2 * ur - q1 * ui
        out[9 + 3 * j + k] = q0 * li - q3 * lr - q2 * ui + q1 * ur
    return out


def third_row(m):
    re, im = list(m[:6]), list(m[6:])
    for k in range(3):
        a, b = (k + 1) % 3, (k + 2) % 3
        re.append(
            m[a] * m[3 + b] - m[6 + a] * m[9 + b] - m[b] * m[3 + a] + m[6 + b] * m[9 + a]
        )
        im.append(
            m[b] * m[9 + a] + m[6 + b] * m[3 + a] - m[a] * m[9 + b] - m[6 + a] * m[3 + b]
        )
    return re + im


def two_rows(m):
    return m[:6] + m[9:15]


PAIRS = ((0, 1), (0, 2), (1, 2))


def kernel(
    sizes,
    links_hbm,
    trans_hbm,
    out_hbm,
    mon_out,
    links,
    g,
    w,
    py,
    pz,
    tsend,
    trecv,
    halo,
    fsend,
    zsend,
    zrecv,
    ysend,
    yrecv,
    mon,
    plane,
    line,
    load_sem,
    t_send_sem,
    t_recv_sem,
    send_sem,
    recv_sem,
    red_send,
    red_recv,
):
    slices, depth, row_len = g.shape[2:]
    nh = row_len // LANES
    half = NX // 2
    strips = LANES // half
    groups = ysend.shape[3]
    last = slices - 1
    steps = 2 * ITERS
    me = {a: lax.axis_index(a) for a in AXES}

    def peer(axis, d):
        n = sizes[axis]
        return {axis: lax.rem(me[axis] + d + n, n)}

    loads = [
        pltpu.make_async_copy(trans_hbm.at[1], g.at[1], load_sem.at[0]),
        pltpu.make_async_copy(links_hbm.at[1], links.at[1], load_sem.at[1]),
        pltpu.make_async_copy(trans_hbm.at[0], g.at[0], load_sem.at[2]),
        pltpu.make_async_copy(links_hbm.at[0], links.at[0], load_sem.at[3]),
    ]
    for copy in loads:
        copy.start()
    barrier = pltpu.get_barrier_semaphore()
    flat = me["gz"] * sizes["gy"] + me["gy"]
    width = sizes["gz"] * sizes["gy"]

    def plane_peer(d):
        other = lax.rem(flat + d, width)
        return {"gz": other // sizes["gy"], "gy": lax.rem(other, sizes["gy"])}

    for d in range(1, sizes["ta"]):
        pl.semaphore_signal(barrier, inc=1, device_id=peer("ta", d), device_id_type=MESH)
    for d in range(1, width):
        pl.semaphore_signal(barrier, inc=1, device_id=plane_peer(d), device_id_type=MESH)
    count = sizes["ta"] + width - 2
    mon[...] = jnp.zeros_like(mon)
    pl.semaphore_wait(barrier, count)

    row = lax.broadcasted_iota(jnp.int32, (depth, LANES), 0)
    lane = lax.broadcasted_iota(jnp.int32, (depth, LANES), 1)
    column = lane % half
    strip = lane // half

    def piece(h):
        return pl.ds(h * LANES if isinstance(h, int) else pl.multiple_of(h * LANES, LANES), LANES)

    def load(ref, *index):
        t, h = index[-2:]
        return [ref[index[:-2] + (comp, t, slice(None), piece(h))] for comp in range(18)]

    def store(ref, values, *index):
        t, h = index[-2:]
        for comp in range(18):
            ref[index[:-2] + (comp, t, slice(None), piece(h))] = values[comp]

    def remote(src, dst, k, number, axis, d):
        return pltpu.make_async_remote_copy(
            src_ref=src,
            dst_ref=dst,
            send_sem=send_sem.at[k, number],
            recv_sem=recv_sem.at[k, number],
            device_id=peer(axis, d),
            device_id_type=MESH,
        )

    def t_copy(slot, way, h):
        return pltpu.make_async_remote_copy(
            src_ref=tsend.at[slot, way, :, :, piece(h)],
            dst_ref=trecv.at[slot, way, :, :, piece(h)],
            send_sem=t_send_sem.at[slot, way, h],
            recv_sem=t_recv_sem.at[slot, way, h],
            device_id=peer("ta", 1 if way else -1),
            device_id_type=MESH,
        )

    def full_copy(way, h):
        return pltpu.make_async_remote_copy(
            src_ref=fsend.at[way, :, :, piece(h)],
            dst_ref=halo.at[0, way, :, :, piece(h)],
            send_sem=t_send_sem.at[steps + 1, way, h],
            recv_sem=t_recv_sem.at[steps + 1, way, h],
            device_id=peer("ta", 1 if way else -1),
            device_id_type=MESH,
        )

    def send_full(way, h):
        values = load(g, 0, last if way else 0, h)
        if way:
            values = mul(values, load(links, 0, 3, last, h))
        put(fsend, (way,), h, values)
        full_copy(way, h).start()

    def side(k):
        return [
            remote(ysend.at[k, 0], yrecv.at[k, 0], k, 2, "gy", -1),
            remote(ysend.at[k, 1], yrecv.at[k, 1], k, 3, "gy", 1),
            remote(zsend.at[k, 0], zrecv.at[k, 0], k, 0, "gz", -1),
            remote(zsend.at[k, 1], zrecv.at[k, 1], k, 1, "gz", 1),
        ]

    def put(ref, index, h, values):
        for number, value in enumerate(values):
            ref[index + (number, slice(None), piece(h))] = value

    def get(ref, index, h, count):
        return [ref[index + (number, slice(None), piece(h))] for number in range(count)]

    def send_given(slot, colour, h):
        put(tsend, (slot, 0), h, two_rows(load(g, colour, 0, h)))
        t_copy(slot, 0, h).start()
        prod = mul(load(g, colour, last, h), load(links, colour, 3, last, h))
        put(tsend, (slot, 1), h, two_rows(prod))
        t_copy(slot, 1, h).start()

    def take_given(slot, colour, way, h):
        t_copy(slot, way, h).wait_recv()
        put(halo, (colour, way), h, third_row(get(trecv, (slot, way), h, 12)))

    def take_turned(slot, colour, way, h):
        t_copy(slot, way, h).wait_recv()
        q = get(trecv, (slot, way), h, 12)
        m = get(halo, (colour, way), h, 18)
        for number, (i, j) in enumerate(PAIRS):
            m = rotate(m, q[4 * number : 4 * number + 4], i, j)
        put(halo, (colour, way), h, m)

    def pack(values, ref, k, way, t):
        for group in range(groups):
            tile = None
            for j in range(strips):
                comp = group * strips + j
                if comp >= 18:
                    continue
                turn = (half * (j + way)) % LANES
                moved = pltpu.roll(values[comp], turn, 1) if turn else values[comp]
                tile = moved if tile is None else jnp.where(strip == j, moved, tile)
            ref[k, way, t, group] = tile

    def unpack(ref, k, way, t):
        out = []
        for comp in range(18):
            group, j = comp // strips, comp % strips
            tile = ref[k, way, t, group]
            turn = (LANES - half - half * j if way == 0 else LANES - half * j) % LANES
            out.append(pltpu.roll(tile, turn, 1) if turn else tile)
        return out

    def products(k, p, t, h, other):
        prod_y = mul(other, load(links, p, 1, t, h))
        store(py, prod_y, t, h)
        if h == 0:
            pack(other, ysend, k, 0, t)
        if h == nh - 1:
            pack(prod_y, ysend, k, 1, t)
        prod_z = mul(other, load(links, p, 2, t, h))
        store(pz, prod_z, t, h)
        for comp in range(18):
            zsend[k, 0, t, comp : comp + 1, piece(h)] = other[comp][0:1]
            zsend[k, 1, t, comp : comp + 1, piece(h)] = prod_z[comp][depth - 1 : depth]

    def half_sweep(n, c):
        p = 1 - c
        k = 2 * n + c
        sides = side(k)
        if c == 0:
            @pl.when(n == 0)
            def _():
                loads[2].wait()
                loads[3].wait()

        def along_x(t, _):
            offset = (row + strip + (t + c)) % 2
            for h in range(nh):
                other = load(g, p, t, h)
                ahead = []
                for v in other:
                    stepped = jnp.where(
                        column == half - 1, pltpu.roll(v, half - 1, 1), pltpu.roll(v, LANES - 1, 1)
                    )
                    ahead.append(jnp.where(offset == 0, v, stepped))
                acc = mul_adj(load(links, c, 0, t, h), ahead)
                behind = []
                for v in mul(other, load(links, p, 0, t, h)):
                    stepped = jnp.where(
                        column == 0, pltpu.roll(v, LANES - half + 1, 1), pltpu.roll(v, 1, 1)
                    )
                    behind.append(jnp.where(offset == 0, stepped, v))
                store(w, add_adj(acc, behind), t, h)
            return 0

        lax.fori_loop(0, slices, along_x, 0)

        def inner_t(h, _):
            for t in range(last):
                near = mul_adj(load(links, c, 3, t, h), load(g, p, t + 1, h))
                store(w, add(load(w, t, h), near), t, h)
                back = mul(load(g, p, t, h), load(links, p, 3, t, h))
                store(w, add_adj(load(w, t + 1, h), back), t + 1, h)
            return 0

        lax.fori_loop(0, nh, inner_t, 0)
        for copy in sides:
            copy.wait_recv()

        def along_yz(t, _):
            for h in range(nh):
                acc = load(w, t, h)
                behind, ahead = [], []
                prod_z = load(pz, t, h)
                other = load(g, p, t, h)
                for comp in range(18):
                    edge = zrecv[k, 0, t, comp : comp + 1, piece(h)]
                    edge = jnp.broadcast_to(edge, (depth, LANES))
                    moved = pltpu.roll(other[comp], depth - 1, 0)
                    ahead.append(jnp.where(row == depth - 1, edge, moved))
                    edge = zrecv[k, 1, t, comp : comp + 1, piece(h)]
                    edge = jnp.broadcast_to(edge, (depth, LANES))
                    behind.append(jnp.where(row == 0, edge, pltpu.roll(prod_z[comp], 1, 0)))
                acc = add_adj(acc, behind)
                acc = add(acc, mul_adj(load(links, c, 2, t, h), ahead))
                if h == nh - 1:
                    edge = unpack(yrecv, k, 0, t)
                else:
                    edge = [pltpu.roll(v, LANES - half, 1) for v in load(g, p, t, h + 1)]
                ahead = [
                    jnp.where(strip == strips - 1, e, pltpu.roll(v, LANES - half, 1))
                    for e, v in zip(edge, other)
                ]
                acc = add(acc, mul_adj(load(links, c, 1, t, h), ahead))
                if h == 0:
                    edge = unpack(yrecv, k, 1, t)
                else:
                    edge = [pltpu.roll(v, half, 1) for v in load(py, t, h - 1)]
                behind = [
                    jnp.where(strip == 0, e, pltpu.roll(v, half, 1))
                    for e, v in zip(edge, load(py, t, h))
                ]
                store(w, add_adj(acc, behind), t, h)
            return 0

        lax.fori_loop(0, slices, along_yz, 0)

        def finish(t, h, acc):
            own = load(g, c, t, h)
            a = mul(own, acc)
            turns = []
            for i, j in PAIRS:
                q = rotation(a, i, j)
                turns.extend(q)
                a = rotate(a, q, i, j)
                own = rotate(own, q, i, j)
            if t == last:
                put(tsend, (k + 1, 1), h, turns)
            if t == 0:
                put(tsend, (k + 1, 0), h, turns)
            store(g, own, c, t, h)
            if c == 1:
                func = a[0] + a[4] + a[8]
                mean = (a[9] + a[13] + a[17]) * (1.0 / 3.0)
                div = None
                for i in range(3):
                    d = a[9 + 4 * i] - mean
                    div = d * d if div is None else div + d * d
                for i, j in ((0, 1), (0, 2), (1, 2)):
                    d = a[3 * i + j] - a[3 * j + i]
                    e = a[9 + 3 * i + j] + a[9 + 3 * j + i]
                    div = div + 0.5 * (d * d + e * e)
                mon[n, 0] += func
                mon[n, 1] += div

        def onward(action):
            if c == 0:
                action()
            else:
                pl.when(k + 1 < steps)(action)

        def pass_on(way, h):
            if c == 0:
                @pl.when(n == 0)
                def _():
                    send_full(way, h)

                @pl.when(n > 0)
                def _():
                    t_copy(k + 1, way, h).start()
            else:
                @pl.when(k + 1 < steps)
                def _():
                    t_copy(k + 1, way, h).start()

        def take(way, h):
            if c == 1:
                @pl.when(n == 0)
                def _():
                    full_copy(way, h).wait_recv()

                @pl.when(n > 0)
                def _():
                    take_turned(k, p, way, h)
            else:
                @pl.when(n == 0)
                def _():
                    take_given(k, p, way, h)

                @pl.when(n > 0)
                def _():
                    take_turned(k, p, way, h)

        for h in range(nh):
            take(0, h)
            edge = get(halo, (p, 0), h, 18)
            finish(last, h, add(load(w, last, h), mul_adj(load(links, c, 3, last, h), edge)))
            pass_on(1, h)
            for t in range(1, last):
                finish(t, h, load(w, t, h))
            take(1, h)
            edge = get(halo, (p, 1), h, 18)
            finish(0, h, add_adj(load(w, 0, h), edge))

            pass_on(0, h)

            def after():
                for t in range(slices):
                    products(k + 1, c, t, h, load(g, c, t, h))
                follow = side(k + 1)
                if h == 0:
                    follow[0].start()
                if h == nh - 1:
                    for copy in follow[1:]:
                        copy.start()

            onward(after)

    loads[0].wait()
    loads[1].wait()
    for h in range(nh):
        send_given(0, 1, h)
    for h in range(nh):
        for t in range(slices):
            products(0, 1, t, h, load(g, 1, t, h))
    for copy in side(0):
        copy.start()

    def iteration(n, _):
        half_sweep(n, 0)
        half_sweep(n, 1)
        return 0

    lax.fori_loop(0, ITERS, iteration, 0)
    store_out = pltpu.make_async_copy(g, out_hbm, load_sem.at[0])
    store_out.start()

    spot = lax.broadcasted_iota(jnp.int32, (1, LANES), 1)
    sums = jnp.zeros((1, LANES), jnp.float32)
    for n in range(ITERS):
        for part in range(2):
            value = jnp.sum(jnp.sum(mon[n, part], axis=0, keepdims=True), axis=1, keepdims=True)
            sums = jnp.where(spot == 2 * n + part, value, sums)

    def exchange(ref, here, size, target, base):
        copies = []
        ref[here] = sums
        for d in range(1, size):
            copy = pltpu.make_async_remote_copy(
                src_ref=ref.at[here],
                dst_ref=ref.at[here],
                send_sem=red_send.at[base + d],
                recv_sem=red_recv.at[base + d],
                device_id=target(d),
                device_id_type=MESH,
            )
            copy.start()
            copies.append(copy)
        for d in range(1, size):
            source = lax.rem(here - d + size, size)
            pltpu.make_async_remote_copy(
                src_ref=ref.at[here],
                dst_ref=ref.at[source],
                send_sem=red_send.at[base + d],
                recv_sem=red_recv.at[base + d],
                device_id=target(d),
                device_id_type=MESH,
            ).wait_recv()
        return total([ref[number] for number in range(size)]), copies

    sums, pending = exchange(plane, flat, width, plane_peer, 0)
    sums, more = exchange(line, me["ta"], sizes["ta"], lambda d: peer("ta", d), width)
    sites = slices * depth * row_len * sizes["ta"] * width
    for n in range(ITERS):
        mon_out[0, n] = 1.0 - sums[0, 2 * n] / (24.0 * sites)
        mon_out[1, n] = sums[0, 2 * n + 1] / float(sites)
    for copy in pending + more:
        copy.wait_send()
    for h in range(nh):
        for way in range(2):
            full_copy(way, h).wait_send()
            for slot in range(steps):
                if slot != 1:
                    t_copy(slot, way, h).wait_send()
    for k in range(steps):
        for copy in side(k):
            copy.wait_send()
    store_out.wait()


def shards(sizes, lattice_links, transform):
    slices, depth, row_len = transform.shape[2:]
    nh = row_len // LANES
    strips = LANES // (NX // 2)
    groups = -(-18 // strips)
    steps = 2 * ITERS
    face = (18, slices, depth, row_len)
    assert depth == 8 and slices > 1 and row_len % LANES == 0
    f32 = jnp.float32
    width = sizes["gz"] * sizes["gy"]
    lines = width + sizes["ta"]
    return pl.pallas_call(
        functools.partial(kernel, sizes),
        out_shape=(
            jax.ShapeDtypeStruct(transform.shape, f32),
            jax.ShapeDtypeStruct((2, ITERS), f32),
        ),
        in_specs=[pl.BlockSpec(memory_space=pltpu.HBM)] * 2,
        out_specs=(
            pl.BlockSpec(memory_space=pl.ANY),
            pl.BlockSpec(memory_space=pltpu.SMEM),
        ),
        scratch_shapes=[
            pltpu.VMEM(lattice_links.shape, f32),
            pltpu.VMEM(transform.shape, f32),
            pltpu.VMEM(face, f32),
            pltpu.VMEM(face, f32),
            pltpu.VMEM(face, f32),
            pltpu.VMEM((steps + 2, 2, 12, depth, row_len), f32),
            pltpu.VMEM((steps + 2, 2, 12, depth, row_len), f32),
            pltpu.VMEM((2, 2, 18, depth, row_len), f32),
            pltpu.VMEM((2, 18, depth, row_len), f32),
            pltpu.VMEM((steps, 2, slices, 18, row_len), f32),
            pltpu.VMEM((steps, 2, slices, 18, row_len), f32),
            pltpu.VMEM((steps, 2, slices, groups, depth, LANES), f32),
            pltpu.VMEM((steps, 2, slices, groups, depth, LANES), f32),
            pltpu.VMEM((ITERS, 2, depth, LANES), f32),
            pltpu.VMEM((width, 1, LANES), f32),
            pltpu.VMEM((sizes["ta"], 1, LANES), f32),
            pltpu.SemaphoreType.DMA((4,)),
            pltpu.SemaphoreType.DMA((steps + 2, 2, nh)),
            pltpu.SemaphoreType.DMA((steps + 2, 2, nh)),
            pltpu.SemaphoreType.DMA((steps, 4)),
            pltpu.SemaphoreType.DMA((steps, 4)),
            pltpu.SemaphoreType.DMA((lines,)),
            pltpu.SemaphoreType.DMA((lines,)),
        ],
        compiler_params=pltpu.CompilerParams(
            collective_id=0, has_side_effects=True, vmem_limit_bytes=67043328
        ),
    )(lattice_links, transform)


def solution(mesh):
    sizes = {axis: mesh.shape[axis] for axis in AXES}
    return jax.shard_map(
        functools.partial(shards, sizes),
        mesh=mesh,
        in_specs=(P(None, None, None, "ta", "gz", "gy"), P(None, None, "ta", "gz", "gy")),
        out_specs=(P(None, None, "ta", "gz", "gy"), P()),
        check_vma=False,
    )
```

profile of v0, /device:TPU:0, one launch (start us, length us, event | category | flops | bytes accessed | tf_op | source)
XLA Modules:
  0.0 42.7 jit_solution(2835784648475643529)
XLA Ops:
  0.6 38.9 %shard_map.41 = (f32[2,18,2,8,256]{4,3,2,1,0:T(8,128)}, f32[2,2]{1,0:T(2,128)}) custom-call(f32[2,4,18,2,8,256]{5,4,3,2,1,0:T(8,128)} %links_hbm.1, f32[2,18,2,8,256]{4,3,2,1,0:T(8,128)} %trans_hbm.1), custom_call_target="tpu_custom_call" | custom-call | tf_op jit(solution)/shard_map/pallas_call | solution.py:563
  39.6 1.9 %copy.6 = f32[2,18,2,8,256]{4,3,2,1,0:T(8,128)} copy(f32[2,18,2,8,256]{4,3,2,1,0:T(8,128)} %get-tuple-element.4) | data formatting | bytes 1179648
  41.5 1.2 %copy.7 = f32[2,2]{1,0:T(2,128)} copy(f32[2,2]{1,0:T(2,128)} %get-tuple-element.5) | data formatting | bytes 32
where the time goes:
time: 42.9 us; the launch traced here: 42.7 us
  Pallas kernels  38.9 us (91%)
  local copies, waits for them, and re-layouts  3.14 us (7%)
  between operations  0.64 us (1%)
    pallas_call x1, Pallas kernels, shards(): pl.pallas_call(functools.partial(kernel, sizes), out_shape=(jax.ShapeDtyp...  38.9 us
    unnamed x2, local copies, waits for them, and re-layouts  3.14 us

commit v1 on v0

--- a/solution.py
+++ b/solution.py
@@ -119,10 +119,9 @@
     sizes,
     links_hbm,
     trans_hbm,
-    out_hbm,
+    g,
     mon_out,
     links,
-    g,
     w,
     py,
     pz,
@@ -136,7 +135,6 @@
     yrecv,
     mon,
     plane,
-    line,
     load_sem,
     t_send_sem,
     t_recv_sem,
@@ -167,20 +165,11 @@
     for copy in loads:
         copy.start()
     barrier = pltpu.get_barrier_semaphore()
-    flat = me["gz"] * sizes["gy"] + me["gy"]
-    width = sizes["gz"] * sizes["gy"]
-
-    def plane_peer(d):
-        other = lax.rem(flat + d, width)
-        return {"gz": other // sizes["gy"], "gy": lax.rem(other, sizes["gy"])}
-
-    for d in range(1, sizes["ta"]):
-        pl.semaphore_signal(barrier, inc=1, device_id=peer("ta", d), device_id_type=MESH)
-    for d in range(1, width):
-        pl.semaphore_signal(barrier, inc=1, device_id=plane_peer(d), device_id_type=MESH)
-    count = sizes["ta"] + width - 2
+    near = [(a, d) for a in AXES for d in sorted({1, sizes[a] - 1})]
+    for axis, d in near:
+        pl.semaphore_signal(barrier, inc=1, device_id=peer(axis, d), device_id_type=MESH)
     mon[...] = jnp.zeros_like(mon)
-    pl.semaphore_wait(barrier, count)
+    pl.semaphore_wait(barrier, len(near))
 
     row = lax.broadcasted_iota(jnp.int32, (depth, LANES), 0)
     lane = lax.broadcasted_iota(jnp.int32, (depth, LANES), 1)
@@ -493,8 +482,6 @@
         return 0
 
     lax.fori_loop(0, ITERS, iteration, 0)
-    store_out = pltpu.make_async_copy(g, out_hbm, load_sem.at[0])
-    store_out.start()
 
     spot = lax.broadcasted_iota(jnp.int32, (1, LANES), 1)
     sums = jnp.zeros((1, LANES), jnp.float32)
@@ -503,40 +490,45 @@
             value = jnp.sum(jnp.sum(mon[n, part], axis=0, keepdims=True), axis=1, keepdims=True)
             sums = jnp.where(spot == 2 * n + part, value, sums)
 
-    def exchange(ref, here, size, target, base):
-        copies = []
-        ref[here] = sums
-        for d in range(1, size):
-            copy = pltpu.make_async_remote_copy(
-                src_ref=ref.at[here],
-                dst_ref=ref.at[here],
-                send_sem=red_send.at[base + d],
-                recv_sem=red_recv.at[base + d],
-                device_id=target(d),
-                device_id_type=MESH,
-            )
-            copy.start()
-            copies.append(copy)
-        for d in range(1, size):
-            source = lax.rem(here - d + size, size)
-            pltpu.make_async_remote_copy(
-                src_ref=ref.at[here],
-                dst_ref=ref.at[source],
-                send_sem=red_send.at[base + d],
-                recv_sem=red_recv.at[base + d],
-                device_id=target(d),
-                device_id_type=MESH,
-            ).wait_recv()
-        return total([ref[number] for number in range(size)]), copies
-
-    sums, pending = exchange(plane, flat, width, plane_peer, 0)
-    sums, more = exchange(line, me["ta"], sizes["ta"], lambda d: peer("ta", d), width)
+    lines = plane.shape[0]
+    here = (me["ta"] * sizes["gz"] + me["gz"]) * sizes["gy"] + me["gy"]
+    plane[here] = sums
+    offsets = [
+        (i, j, k)
+        for i in range(sizes["ta"])
+        for j in range(sizes["gz"])
+        for k in range(sizes["gy"])
+        if i or j or k
+    ]
+
+    def to_other(i, j, k):
+        return pltpu.make_async_remote_copy(
+            src_ref=plane.at[here],
+            dst_ref=plane.at[here],
+            send_sem=red_send,
+            recv_sem=red_recv,
+            device_id=peer("ta", i) | peer("gz", j) | peer("gy", k),
+            device_id_type=MESH,
+        )
+
+    for offset in reversed(offsets):
+        to_other(*offset).start()
+    width = sizes["gz"] * sizes["gy"]
+    arrivals = pltpu.make_async_remote_copy(
+        src_ref=plane.at[pl.ds(0, lines - 1)],
+        dst_ref=plane.at[pl.ds(0, lines - 1)],
+        send_sem=red_send,
+        recv_sem=red_recv,
+        device_id=peer("ta", 1),
+        device_id_type=MESH,
+    )
+    arrivals.wait_recv()
+    sums = total([plane[number] for number in range(lines)])
     sites = slices * depth * row_len * sizes["ta"] * width
     for n in range(ITERS):
         mon_out[0, n] = 1.0 - sums[0, 2 * n] / (24.0 * sites)
         mon_out[1, n] = sums[0, 2 * n + 1] / float(sites)
-    for copy in pending + more:
-        copy.wait_send()
+    arrivals.wait_send()
     for h in range(nh):
         for way in range(2):
             full_copy(way, h).wait_send()
@@ -546,7 +538,6 @@
     for k in range(steps):
         for copy in side(k):
             copy.wait_send()
-    store_out.wait()
 
 
 def shards(sizes, lattice_links, transform):
@@ -559,21 +550,20 @@
     assert depth == 8 and slices > 1 and row_len % LANES == 0
     f32 = jnp.float32
     width = sizes["gz"] * sizes["gy"]
-    lines = width + sizes["ta"]
-    return pl.pallas_call(
+    lines = width * sizes["ta"]
+    g, mon = pl.pallas_call(
         functools.partial(kernel, sizes),
         out_shape=(
-            jax.ShapeDtypeStruct(transform.shape, f32),
-            jax.ShapeDtypeStruct((2, ITERS), f32),
+            pltpu.VMEM(transform.shape, f32),
+            pltpu.SMEM((2, ITERS), f32),
         ),
         in_specs=[pl.BlockSpec(memory_space=pltpu.HBM)] * 2,
         out_specs=(
-            pl.BlockSpec(memory_space=pl.ANY),
+            pl.BlockSpec(memory_space=pltpu.VMEM),
             pl.BlockSpec(memory_space=pltpu.SMEM),
         ),
         scratch_shapes=[
             pltpu.VMEM(lattice_links.shape, f32),
-            pltpu.VMEM(transform.shape, f32),
             pltpu.VMEM(face, f32),
             pltpu.VMEM(face, f32),
             pltpu.VMEM(face, f32),
@@ -586,20 +576,39 @@
             pltpu.VMEM((steps, 2, slices, groups, depth, LANES), f32),
             pltpu.VMEM((steps, 2, slices, groups, depth, LANES), f32),
             pltpu.VMEM((ITERS, 2, depth, LANES), f32),
-            pltpu.VMEM((width, 1, LANES), f32),
-            pltpu.VMEM((sizes["ta"], 1, LANES), f32),
+            pltpu.VMEM((lines, 1, LANES), f32),
             pltpu.SemaphoreType.DMA((4,)),
             pltpu.SemaphoreType.DMA((steps + 2, 2, nh)),
             pltpu.SemaphoreType.DMA((steps + 2, 2, nh)),
             pltpu.SemaphoreType.DMA((steps, 4)),
             pltpu.SemaphoreType.DMA((steps, 4)),
-            pltpu.SemaphoreType.DMA((lines,)),
-            pltpu.SemaphoreType.DMA((lines,)),
+            pltpu.SemaphoreType.DMA,
+            pltpu.SemaphoreType.DMA,
         ],
         compiler_params=pltpu.CompilerParams(
-            collective_id=0, has_side_effects=True, vmem_limit_bytes=67043328
+            collective_id=0, has_side_effects=True, vmem_limit_bytes=67043328 - 900000 // 4096 * 4096
         ),
     )(lattice_links, transform)
+
+    def finish(g_ref, mon_ref, out_ref, mon_out, sem, sem2):
+        copy = pltpu.make_async_copy(g_ref, out_ref, sem)
+        copy.start()
+        small = pltpu.make_async_copy(mon_ref, mon_out, sem2)
+        small.start()
+        copy.wait()
+        small.wait()
+
+    return pl.pallas_call(
+        finish,
+        out_shape=(
+            jax.ShapeDtypeStruct(transform.shape, f32),
+            jax.ShapeDtypeStruct((2, ITERS), f32),
+        ),
+        in_specs=[pl.BlockSpec(memory_space=pltpu.VMEM), pl.BlockSpec(memory_space=pltpu.SMEM)],
+        out_specs=(pl.BlockSpec(memory_space=pltpu.HBM), pl.BlockSpec(memory_space=pltpu.HBM)),
+        scratch_shapes=[pltpu.SemaphoreType.DMA,pltpu.SemaphoreType.DMA],
+        compiler_params=pltpu.CompilerParams(vmem_limit_bytes=1 << 20),
+    )(g, mon)
 
 
 def solution(mesh):

time: 42.9 us -> 38 us (0.89)
  local copies, waits for them, and re-layouts: 3.14 us -> 0 us
  Pallas kernels: 38.9 us -> 37.2 us
    unnamed x2 -> x0, local copies, waits for them, and re-layouts: 3.14 us -> none
    pallas_call x1 -> x2, Pallas kernels: 38.9 us -> 37.2 us  [the longest x1 36.3 us: shards(): pl.pallas_call(functools.partial(kernel, sizes), out_shape=(pltpu.VMEM(tr...]
where the time goes in v1:
time: 38 us; the launch traced here: 37.8 us
  Pallas kernels  37.2 us (98%)
  between operations  0.64 us (2%)
    pallas_call x1, Pallas kernels, shards(): pl.pallas_call(functools.partial(kernel, sizes), out_shape=(pltpu.VMEM(tr...  36.3 us
    pallas_call x1, Pallas kernels, shards(): pl.pallas_call(finish, out_shape=(jax.ShapeDtypeStruct(transform.shape, f...  0.84 us

profile of v1, /device:TPU:0, one launch (start us, length us, event | category | flops | bytes accessed | tf_op | source)
XLA Modules:
  0.0 37.8 jit_solution(9803082504532249936)
XLA Ops:
  0.6 36.3 %shard_map.41 = (f32[2,18,2,8,256]{4,3,2,1,0:T(8,128)S(1)}, f32[2,2]{1,0:T(2,128)S(4)}) custom-call(f32[2,4,18,2,8,256]{5,4,3,2,1,0:T(8,128)} %links_hbm.1, f32[2,18,2,8,256]{4,3,2,1,0:T(8,128)} %trans_hbm.1), custom_call_target="tpu_custom_call" | custom-call | tf_op jit(solution)/shard_map/pallas_call | solution.py:554
  37.0 0.8 %shard_map.42 = (f32[2,18,2,8,256]{4,3,2,1,0:T(8,128)}, f32[2,2]{1,0:T(2,128)}) custom-call(f32[2,18,2,8,256]{4,3,2,1,0:T(8,128)S(1)} %get-tuple-element.4.g_ref, f32[2,2]{1,0:T(2,128)S(4)} %get-tuple-element.5.mon_ref), custom_call_target="tpu_custom_call" | custom-call | tf_op jit(solution)/shard_map/pallas_call | solution.py:601

commit v2 on v1

v2 whole, which is shorter than its diff:
```python
import functools

import jax
import jax.numpy as jnp
from jax import lax
from jax.experimental import pallas as pl
from jax.experimental.pallas import tpu as pltpu
from jax.sharding import PartitionSpec as P

NX = 64
ITERS = 2
OMEGA = 1.7
GUARD = 1e-12
FLOOR = 1e-20
FAR = 1e15
LANES = 128
AXES = ("ta", "gz", "gy")
MESH = pl.DeviceIdType.MESH


def total(terms):
    out = terms[0]
    for term in terms[1:]:
        out = out + term
    return out


def mul(a, b):
    re, im = [], []
    for i in range(3):
        for j in range(3):
            re.append(
                total([a[3 * i + k] * b[3 * k + j] for k in range(3)])
                - total([a[9 + 3 * i + k] * b[9 + 3 * k + j] for k in range(3)])
            )
            im.append(
                total([a[3 * i + k] * b[9 + 3 * k + j] for k in range(3)])
                + total([a[9 + 3 * i + k] * b[3 * k + j] for k in range(3)])
            )
    return re + im


def mul_adj(a, b):
    re, im = [], []
    for i in range(3):
        for j in range(3):
            re.append(
                total([a[3 * i + k] * b[3 * j + k] for k in range(3)])
                + total([a[9 + 3 * i + k] * b[9 + 3 * j + k] for k in range(3)])
            )
            im.append(
                total([a[9 + 3 * i + k] * b[3 * j + k] for k in range(3)])
                - total([a[3 * i + k] * b[9 + 3 * j + k] for k in range(3)])
            )
    return re + im


def add(a, b):
    return [x + y for x, y in zip(a, b)]


def add_adj(a, b):
    out = []
    for i in range(3):
        for j in range(3):
            out.append(a[3 * i + j] + b[3 * j + i])
    for i in range(3):
        for j in range(3):
            out.append(a[9 + 3 * i + j] - b[9 + 3 * j + i])
    return out


def rotation(a, i, j):
    ii, jj, ij, ji = 4 * i, 4 * j, 3 * i + j, 3 * j + i
    v0 = a[ii] + a[jj]
    v1 = -(a[9 + ij] + a[9 + ji])
    v2 = a[ji] - a[ij]
    v3 = a[9 + jj] - a[9 + ii]
    tail = v1 * v1 + v2 * v2 + v3 * v3
    length = jnp.sqrt(v0 * v0 + tail)
    s0 = (1.0 - OMEGA) * length + OMEGA * v0
    inv = lax.rsqrt(s0 * s0 + (OMEGA * OMEGA) * tail + GUARD)
    scaled = OMEGA * inv
    return (s0 * inv, v1 * scaled, v2 * scaled, v3 * scaled)


def rotate(m, q, i, j):
    q0, q1, q2, q3 = q
    out = list(m)
    for k in range(3):
        ur, ui = m[3 * i + k], m[9 + 3 * i + k]
        lr, li = m[3 * j + k], m[9 + 3 * j + k]
        out[3 * i + k] = q0 * ur - q3 * ui + q2 * lr - q1 * li
        out[9 + 3 * i + k] = q0 * ui + q3 * ur + q2 * li + q1 * lr
        out[3 * j + k] = q0 * lr + q3 * li - q2 * ur - q1 * ui
        out[9 + 3 * j + k] = q0 * li - q3 * lr - q2 * ui + q1 * ur
    return out


def third_row(m):
    re, im = list(m[:6]), list(m[6:])
    for k in range(3):
        a, b = (k + 1) % 3, (k + 2) % 3
        re.append(
            m[a] * m[3 + b] - m[6 + a] * m[9 + b] - m[b] * m[3 + a] + m[6 + b] * m[9 + a]
        )
        im.append(
            m[b] * m[9 + a] + m[6 + b] * m[3 + a] - m[a] * m[9 + b] - m[6 + a] * m[3 + b]
        )
    return re + im


def to_flat(x, v):
    square = total([c * c for c in v])
    scale = jnp.where(x >= 0.0, 1.0 + x, square / (1.0 + jnp.abs(x)))
    pole = scale < FLOOR
    inv = 1.0 / jnp.where(pole, 1.0, scale)
    flat = [c * inv for c in v]
    return [jnp.where(pole, FAR, flat[0])] + [jnp.where(pole, 0.0, c) for c in flat[1:]]


def from_flat(flat):
    scale = 2.0 / (1.0 + total([c * c for c in flat]))
    return [scale - 1.0] + [c * scale for c in flat]


def cmul(a, b):
    return (a[0] * b[0] - a[1] * b[1], a[0] * b[1] + a[1] * b[0])


def cmul_conj(a, b):
    return (a[0] * b[0] + a[1] * b[1], a[1] * b[0] - a[0] * b[1])


def first_row(flat):
    r0, i0, r1, i1, r2, i2 = from_flat(flat)
    square = r0 * r0 + i0 * i0 + r1 * r1 + i1 * i1
    small = square < FLOOR
    inv = lax.rsqrt(jnp.where(small, 1.0, square))
    c0 = (jnp.where(small, 1.0, r0 * inv), jnp.where(small, 0.0, i0 * inv))
    c1 = (jnp.where(small, 0.0, r1 * inv), jnp.where(small, 0.0, i1 * inv))
    norm = jnp.where(small, 0.0, square * inv)
    return [r0, r1, r2], [i0, i1, i2], c0, c1, norm


def encode(m):
    flat = to_flat(m[0], [m[9], m[1], m[10], m[2], m[11]])
    re, im, c0, c1, norm = first_row(flat)
    a2 = (re[2], im[2])
    b0, b1, b2 = [(m[3 + k], m[12 + k]) for k in range(3)]
    x, y = cmul(b1, c0), cmul(b0, c1)
    u, v = cmul_conj(b0, c0), cmul_conj(b1, c1)
    w = cmul(a2, (u[0] + v[0], u[1] + v[1]))
    return flat + to_flat(
        x[0] - y[0], [x[1] - y[1], norm * b2[0] - w[0], norm * b2[1] - w[1]]
    )


def decode(values):
    re, im, c0, c1, norm = first_row(values[:5])
    p0, p1, r0, r1 = from_flat(values[5:])
    p, r = (p0, p1), (r0, r1)
    turn = cmul_conj(r, (re[2], im[2]))
    x, y = cmul_conj(p, c1), cmul(turn, c0)
    u, v = cmul_conj(p, c0), cmul(turn, c1)
    return third_row(
        re + [-x[0] - y[0], u[0] - v[0], norm * r0]
        + im + [-x[1] - y[1], u[1] - v[1], norm * r1]
    )


PAIRS = ((0, 1), (0, 2), (1, 2))


def kernel(
    sizes,
    links_hbm,
    trans_hbm,
    g,
    mon_out,
    links,
    w,
    cb,
    py,
    pz,
    tsend,
    trecv,
    halo,
    esend,
    erecv,
    zsend,
    zrecv,
    ysend,
    yrecv,
    mon,
    plane,
    load_sem,
    t_send_sem,
    t_recv_sem,
    first_send_sem,
    first_recv_sem,
    side_send_sem,
    side_recv_sem,
    red_send,
    red_recv,
):
    slices, depth, row_len = g.shape[2:]
    nh = row_len // LANES
    half = NX // 2
    strips = LANES // half
    groups = ysend.shape[3]
    last = slices - 1
    steps = 2 * ITERS
    me = {a: lax.axis_index(a) for a in AXES}

    def peer(axis, d):
        n = sizes[axis]
        return {axis: lax.rem(me[axis] + d + n, n)}

    loads = [
        pltpu.make_async_copy(src, dst, load_sem.at[number])
        for number, (src, dst) in enumerate(
            [
                (trans_hbm.at[1], g.at[1]),
                (links_hbm.at[1, 3], links.at[1, 3]),
                (links_hbm.at[1, pl.ds(1, 2)], links.at[1, pl.ds(1, 2)]),
                (trans_hbm.at[0], g.at[0]),
                (links_hbm.at[0, 3], links.at[0, 3]),
                (links_hbm.at[1, 0], links.at[1, 0]),
                (links_hbm.at[0, pl.ds(0, 3)], links.at[0, pl.ds(0, 3)]),
            ]
        )
    ]
    for copy in loads:
        copy.start()
    barrier = pltpu.get_barrier_semaphore()
    near = [(a, d) for a in AXES for d in sorted({1, sizes[a] - 1})]
    for axis, d in near:
        pl.semaphore_signal(barrier, inc=1, device_id=peer(axis, d), device_id_type=MESH)
    mon[...] = jnp.zeros_like(mon)
    pl.semaphore_wait(barrier, len(near))

    row = lax.broadcasted_iota(jnp.int32, (depth, LANES), 0)
    lane = lax.broadcasted_iota(jnp.int32, (depth, LANES), 1)
    column = lane % half
    strip = lane // half
    flip = (me["ta"] + 1) // sizes["ta"]

    def piece(h):
        return pl.ds(h * LANES if isinstance(h, int) else pl.multiple_of(h * LANES, LANES), LANES)

    def load(ref, *index):
        t, h = index[-2:]
        return [ref[index[:-2] + (comp, t, slice(None), piece(h))] for comp in range(18)]

    def store(ref, values, *index):
        t, h = index[-2:]
        for comp in range(18):
            ref[index[:-2] + (comp, t, slice(None), piece(h))] = values[comp]

    def put(ref, index, h, values):
        for number, value in enumerate(values):
            ref[index + (number, slice(None), piece(h))] = value

    def get(ref, index, h, count):
        return [ref[index + (number, slice(None), piece(h))] for number in range(count)]

    def along_t(way):
        return {"ta": lax.rem(me["ta"] + 2 * way - 1 + sizes["ta"], sizes["ta"])}

    def t_copy(slot, way, h):
        return pltpu.make_async_remote_copy(
            src_ref=tsend.at[slot, way, :, :, piece(h)],
            dst_ref=trecv.at[slot, way, :, :, piece(h)],
            send_sem=t_send_sem.at[slot, way, h],
            recv_sem=t_recv_sem.at[slot, way, h],
            device_id=along_t(way),
            device_id_type=MESH,
        )

    def first_copy(colour, way, h):
        return pltpu.make_async_remote_copy(
            src_ref=esend.at[colour, way, :, :, piece(h)],
            dst_ref=erecv.at[colour, way, :, :, piece(h)],
            send_sem=first_send_sem.at[colour, way, h],
            recv_sem=first_recv_sem.at[colour, way, h],
            device_id=along_t(way),
            device_id_type=MESH,
        )

    def send_first(colour, way, h):
        values = load(g, colour, last if way else 0, h)
        if way:
            values = mul(values, load(links, colour, 3, last, h))
        put(esend, (colour, way), h, encode(values))
        first_copy(colour, way, h).start()

    def take_first(colour, way, h):
        first_copy(colour, way, h).wait_recv()
        m = decode(get(erecv, (colour, way), h, 8))
        put(halo, (colour, way), h, m)
        return m

    def side(k, t):
        ends = [(zsend, zrecv, "gz"), (ysend, yrecv, "gy")]
        return [
            pltpu.make_async_remote_copy(
                src_ref=src.at[k, way, t],
                dst_ref=dst.at[k, way, t],
                send_sem=side_send_sem.at[k, 2 * number + way, t],
                recv_sem=side_recv_sem.at[k, 2 * number + way, t],
                device_id=peer(axis, 1 if way else -1),
                device_id_type=MESH,
            )
            for number, (src, dst, axis) in enumerate(ends)
            for way in range(2)
        ]

    def pack(values, ref, k, way, t):
        for group in range(groups):
            tile = None
            for j in range(strips):
                comp = group * strips + j
                if comp >= 18:
                    continue
                turn = (half * (j + way)) % LANES
                moved = pltpu.roll(values[comp], turn, 1) if turn else values[comp]
                tile = moved if tile is None else jnp.where(strip == j, moved, tile)
            ref[k, way, t, group] = tile

    def unpack(ref, k, way, t):
        out = []
        for comp in range(18):
            group, j = comp // strips, comp % strips
            tile = ref[k, way, t, group]
            turn = (LANES - half - half * j if way == 0 else LANES - half * j) % LANES
            out.append(pltpu.roll(tile, turn, 1) if turn else tile)
        return out

    def products(k, p, t, h, other):
        prod_y = mul(other, load(links, p, 1, t, h))
        store(py, prod_y, t, h)
        if h == 0:
            pack(other, ysend, k, 0, t)
        if h == nh - 1:
            pack(prod_y, ysend, k, 1, t)
        prod_z = mul(other, load(links, p, 2, t, h))
        store(pz, prod_z, t, h)
        for comp in range(18):
            zsend[k, 0, t, comp : comp + 1, piece(h)] = other[comp][0:1]
            zsend[k, 1, t, comp : comp + 1, piece(h)] = prod_z[comp][depth - 1 : depth]

    def turn_own(k, c, t, way, h):
        q = get(tsend, (k, way), h, 12)
        own = load(g, c, t, h)
        for number, (i, j) in enumerate(PAIRS):
            own = rotate(own, q[4 * number : 4 * number + 4], i, j)
        store(g, own, c, t, h)
        return own

    def half_sweep(n, c):
        p = 1 - c
        k = 2 * n + c
        if c == 0:
            @pl.when(n == 0)
            def _():
                for copy in loads[5:]:
                    copy.wait()

        def inside(h, _):
            for t in range(slices):
                offset = (row + strip + (t + c)) % 2
                other = load(g, p, t, h)
                ahead = []
                for v in other:
                    stepped = jnp.where(
                        column == half - 1, pltpu.roll(v, half - 1, 1), pltpu.roll(v, LANES - 1, 1)
                    )
                    ahead.append(jnp.where(offset == 0, v, stepped))
                acc = mul_adj(load(links, c, 0, t, h), ahead)
                behind = []
                for v in mul(other, load(links, p, 0, t, h)):
                    stepped = jnp.where(
                        column == 0, pltpu.roll(v, LANES - half + 1, 1), pltpu.roll(v, 1, 1)
                    )
                    behind.append(jnp.where(offset == 0, stepped, v))
                acc = add_adj(acc, behind)
                if t < last:
                    acc = add(acc, mul_adj(load(links, c, 3, t, h), load(g, p, t + 1, h)))
                if t > 0:
                    acc = add_adj(acc, mul(load(g, p, t - 1, h), load(links, p, 3, t - 1, h)))
                store(w, acc, t, h)

            def outer():
                return (
                    mul(load(g, c, last, h), load(links, c, 3, last, h)),
                    load(g, c, 0, h),
                )

            def turned_halo(way):
                m = get(halo, (p, way), h, 18)
                q = get(trecv, (k - 3, way), h, 12)
                for number, (i, j) in enumerate(PAIRS):
                    m = rotate(m, q[4 * number : 4 * number + 4], i, j)
                put(halo, (p, way), h, m)
                return m

            def prepare(*halos):
                for way, values in enumerate(outer()):
                    if halos:
                        values = mul_adj(halos[0](way), values)
                    put(cb, (way,), h, values)

            if c == 0:
                pl.when(n == 0)(lambda: prepare())
                pl.when(n == 1)(lambda: prepare(lambda way: get(halo, (p, way), h, 18)))
                if ITERS > 2:
                    pl.when(n > 1)(lambda: prepare(turned_halo))
            else:
                pl.when(n == 0)(lambda: prepare(lambda way: take_first(p, way, h)))
                pl.when(n > 0)(lambda: prepare(turned_halo))
            return 0

        lax.fori_loop(0, nh, inside, 0)

        def along_yz(t, h):
            acc = load(w, t, h)
            behind, ahead = [], []
            prod_z = load(pz, t, h)
            other = load(g, p, t, h)
            for comp in range(18):
                edge = zrecv[k, 0, t, comp : comp + 1, piece(h)]
                edge = jnp.broadcast_to(edge, (depth, LANES))
                moved = pltpu.roll(other[comp], depth - 1, 0)
                ahead.append(jnp.where(row == depth - 1, edge, moved))
                edge = zrecv[k, 1, t, comp : comp + 1, piece(h)]
                edge = jnp.broadcast_to(edge, (depth, LANES))
                behind.append(jnp.where(row == 0, edge, pltpu.roll(prod_z[comp], 1, 0)))
            acc = add_adj(acc, behind)
            acc = add(acc, mul_adj(load(links, c, 2, t, h), ahead))
            if h == nh - 1:
                edge = unpack(yrecv, k, 0, t)
            else:
                edge = [pltpu.roll(v, LANES - half, 1) for v in load(g, p, t, h + 1)]
            ahead = [
                jnp.where(strip == strips - 1, e, pltpu.roll(v, LANES - half, 1))
                for e, v in zip(edge, other)
            ]
            acc = add(acc, mul_adj(load(links, c, 1, t, h), ahead))
            if h == 0:
                edge = unpack(yrecv, k, 1, t)
            else:
                edge = [pltpu.roll(v, half, 1) for v in load(py, t, h - 1)]
            behind = [
                jnp.where(strip == 0, e, pltpu.roll(v, half, 1))
                for e, v in zip(edge, load(py, t, h))
            ]
            acc = add_adj(acc, behind)
            store(w, mul(load(g, c, t, h), acc), t, h)

        def take(way, h):
            def turn():
                t_copy(k - 1, way, h).wait_recv()
                q = get(trecv, (k - 1, way), h, 12)
                m = get(cb, (way,), h, 18)
                for number, (i, j) in enumerate(PAIRS):
                    m = rotate(m, q[4 * number : 4 * number + 4], i, j)
                put(cb, (way,), h, m)

            if c == 1:
                turn()
                return

            @pl.when(n == 0)
            def _():
                put(cb, (way,), h, mul_adj(take_first(p, way, h), get(cb, (way,), h, 18)))

            pl.when(n > 0)(turn)

        def monitor(a):
            func = a[0] + a[4] + a[8]
            mean = (a[9] + a[13] + a[17]) * (1.0 / 3.0)
            div = None
            for i in range(3):
                d = a[9 + 4 * i] - mean
                div = d * d if div is None else div + d * d
            for i, j in PAIRS:
                d = a[3 * i + j] - a[3 * j + i]
                e = a[9 + 3 * i + j] + a[9 + 3 * j + i]
                div = div + 0.5 * (d * d + e * e)
            mon[n, 0] += func
            mon[n, 1] += div

        def slab(number, _):
            back = (number + flip) % 2
            ahead = 1 - back
            t = ahead * last
            for copy in side(k, t):
                copy.wait_recv()
            for h in range(nh):
                along_yz(t, h)
            for h in range(nh):
                take(back, h)
                a = add_adj(load(w, t, h), get(cb, (back,), h, 18))
                turns = []
                for i, j in PAIRS:
                    q = rotation(a, i, j)
                    turns.extend(q)
                    a = rotate(a, q, i, j)
                put(tsend, (k, ahead), h, turns)

                if c == 0:
                    t_copy(k, ahead, h).start()
                    products(k + 1, c, t, h, turn_own(k, c, t, ahead, h))
                else:
                    @pl.when(k + 1 < steps)
                    def _():
                        t_copy(k, ahead, h).start()

                    monitor(a)

                    @pl.when(k + 1 < steps)
                    def _():
                        products(k + 1, c, t, h, turn_own(k, c, t, ahead, h))

            def follow():
                for copy in side(k + 1, t):
                    copy.start()

            if c == 0:
                follow()
            else:
                pl.when(k + 1 < steps)(follow)
            return 0

        lax.fori_loop(0, slices, slab, 0)

    for way in range(2):
        loads[way].wait()
        for h in range(nh):
            send_first(1, way, h)
    loads[2].wait()
    for t in range(slices):
        for h in range(nh):
            products(0, 1, t, h, load(g, 1, t, h))
        for copy in side(0, t):
            copy.start()

    for way in range(2):
        loads[3 + way].wait()
        for h in range(nh):
            send_first(0, way, h)

    def iteration(n, _):
        half_sweep(n, 0)
        half_sweep(n, 1)
        return 0

    lax.fori_loop(0, ITERS, iteration, 0)

    spot = lax.broadcasted_iota(jnp.int32, (1, LANES), 1)
    sums = jnp.zeros((1, LANES), jnp.float32)
    for n in range(ITERS):
        for part in range(2):
            value = jnp.sum(jnp.sum(mon[n, part], axis=0, keepdims=True), axis=1, keepdims=True)
            sums = jnp.where(spot == 2 * n + part, value, sums)

    lines = plane.shape[0]
    here = (me["ta"] * sizes["gz"] + me["gz"]) * sizes["gy"] + me["gy"]
    plane[here] = sums
    offsets = [
        (i, j, k)
        for i in range(sizes["ta"])
        for j in range(sizes["gz"])
        for k in range(sizes["gy"])
        if i or j or k
    ]

    def to_other(i, j, k):
        return pltpu.make_async_remote_copy(
            src_ref=plane.at[here],
            dst_ref=plane.at[here],
            send_sem=red_send,
            recv_sem=red_recv,
            device_id=peer("ta", i) | peer("gz", j) | peer("gy", k),
            device_id_type=MESH,
        )

    for offset in reversed(offsets):
        to_other(*offset).start()
    width = sizes["gz"] * sizes["gy"]
    arrivals = pltpu.make_async_remote_copy(
        src_ref=plane.at[pl.ds(0, lines - 1)],
        dst_ref=plane.at[pl.ds(0, lines - 1)],
        send_sem=red_send,
        recv_sem=red_recv,
        device_id=peer("ta", 1),
        device_id_type=MESH,
    )
    for t in range(slices):
        for h in range(nh):
            turn_own(steps - 1, 1, t, t, h)
    arrivals.wait_recv()
    sums = total([plane[number] for number in range(lines)])
    sites = slices * depth * row_len * sizes["ta"] * width
    for n in range(ITERS):
        mon_out[0, n] = 1.0 - sums[0, 2 * n] / (24.0 * sites)
        mon_out[1, n] = sums[0, 2 * n + 1] / float(sites)
    arrivals.wait_send()
    for h in range(nh):
        for way in range(2):
            for colour in range(2):
                first_copy(colour, way, h).wait_send()
            for k in range(steps - 1):
                t_copy(k, way, h).wait_send()
    for k in range(steps):
        for t in range(slices):
            for copy in side(k, t):
                copy.wait_send()


def shards(sizes, lattice_links, transform):
    slices, depth, row_len = transform.shape[2:]
    nh = row_len // LANES
    strips = LANES // (NX // 2)
    groups = -(-18 // strips)
    steps = 2 * ITERS
    face = (18, slices, depth, row_len)
    assert depth == 8 and slices == 2 and row_len % LANES == 0
    f32 = jnp.float32
    width = sizes["gz"] * sizes["gy"]
    lines = width * sizes["ta"]
    g, mon = pl.pallas_call(
        functools.partial(kernel, sizes),
        out_shape=(
            pltpu.VMEM(transform.shape, f32),
            pltpu.SMEM((2, ITERS), f32),
        ),
        in_specs=[pl.BlockSpec(memory_space=pltpu.HBM)] * 2,
        out_specs=(
            pl.BlockSpec(memory_space=pltpu.VMEM),
            pl.BlockSpec(memory_space=pltpu.SMEM),
        ),
        scratch_shapes=[
            pltpu.VMEM(lattice_links.shape, f32),
            pltpu.VMEM(face, f32),
            pltpu.VMEM((2, 18, depth, row_len), f32),
            pltpu.VMEM(face, f32),
            pltpu.VMEM(face, f32),
            pltpu.VMEM((steps, 2, 12, depth, row_len), f32),
            pltpu.VMEM((steps, 2, 12, depth, row_len), f32),
            pltpu.VMEM((2, 2, 18, depth, row_len), f32),
            pltpu.VMEM((2, 2, 8, depth, row_len), f32),
            pltpu.VMEM((2, 2, 8, depth, row_len), f32),
            pltpu.VMEM((steps, 2, slices, 18, row_len), f32),
            pltpu.VMEM((steps, 2, slices, 18, row_len), f32),
            pltpu.VMEM((steps, 2, slices, groups, depth, LANES), f32),
            pltpu.VMEM((steps, 2, slices, groups, depth, LANES), f32),
            pltpu.VMEM((ITERS, 2, depth, LANES), f32),
            pltpu.VMEM((lines, 1, LANES), f32),
            pltpu.SemaphoreType.DMA((7,)),
            pltpu.SemaphoreType.DMA((steps - 1, 2, nh)),
            pltpu.SemaphoreType.DMA((steps - 1, 2, nh)),
            pltpu.SemaphoreType.DMA((2, 2, nh)),
            pltpu.SemaphoreType.DMA((2, 2, nh)),
            pltpu.SemaphoreType.DMA((steps, 4, slices)),
            pltpu.SemaphoreType.DMA((steps, 4, slices)),
            pltpu.SemaphoreType.DMA,
            pltpu.SemaphoreType.DMA,
        ],
        compiler_params=pltpu.CompilerParams(
            collective_id=0, has_side_effects=True, vmem_limit_bytes=67043328 - 900000 // 4096 * 4096
        ),
    )(lattice_links, transform)

    def finish(g_ref, mon_ref, out_ref, mon_out, sem, sem2):
        copy = pltpu.make_async_copy(g_ref, out_ref, sem)
        copy.start()
        small = pltpu.make_async_copy(mon_ref, mon_out, sem2)
        small.start()
        copy.wait()
        small.wait()

    return pl.pallas_call(
        finish,
        out_shape=(
            jax.ShapeDtypeStruct(transform.shape, f32),
            jax.ShapeDtypeStruct((2, ITERS), f32),
        ),
        in_specs=[pl.BlockSpec(memory_space=pltpu.VMEM), pl.BlockSpec(memory_space=pltpu.SMEM)],
        out_specs=(pl.BlockSpec(memory_space=pltpu.HBM), pl.BlockSpec(memory_space=pltpu.HBM)),
        scratch_shapes=[pltpu.SemaphoreType.DMA,pltpu.SemaphoreType.DMA],
        compiler_params=pltpu.CompilerParams(vmem_limit_bytes=1 << 20),
    )(g, mon)


def solution(mesh):
    sizes = {axis: mesh.shape[axis] for axis in AXES}
    return jax.shard_map(
        functools.partial(shards, sizes),
        mesh=mesh,
        in_specs=(P(None, None, None, "ta", "gz", "gy"), P(None, None, "ta", "gz", "gy")),
        out_specs=(P(None, None, "ta", "gz", "gy"), P()),
        check_vma=False,
    )
```

time: 38 us -> 35.4 us (0.932)
  Pallas kernels: 37.2 us -> 34.6 us
    pallas_call x1, Pallas kernels: 36.3 us -> 33.7 us  [shards(): pl.pallas_call(functools.partial(kernel, sizes), out_shape=(pltpu.VMEM(tr...]
where the time goes in v2:
time: 35.4 us; the launch traced here: 35.2 us
  Pallas kernels  34.6 us (98%)
  between operations  0.64 us (2%)
    pallas_call x1, Pallas kernels, shards(): pl.pallas_call(functools.partial(kernel, sizes), out_shape=(pltpu.VMEM(tr...  33.7 us
    pallas_call x1, Pallas kernels, shards(): pl.pallas_call(finish, out_shape=(jax.ShapeDtypeStruct(transform.shape, f...  0.84 us

profile of v2, /device:TPU:0, one launch (start us, length us, event | category | flops | bytes accessed | tf_op | source)
XLA Modules:
  0.0 35.2 jit_solution(2732692274627472663)
XLA Ops:
  0.6 33.7 %shard_map.41 = (f32[2,18,2,8,256]{4,3,2,1,0:T(8,128)S(1)}, f32[2,2]{1,0:T(2,128)S(4)}) custom-call(f32[2,4,18,2,8,256]{5,4,3,2,1,0:T(8,128)} %links_hbm.1, f32[2,18,2,8,256]{4,3,2,1,0:T(8,128)} %trans_hbm.1), custom_call_target="tpu_custom_call" | custom-call | tf_op jit(solution)/shard_map/pallas_call | solution.py:633
  34.4 0.8 %shard_map.42 = (f32[2,18,2,8,256]{4,3,2,1,0:T(8,128)}, f32[2,2]{1,0:T(2,128)}) custom-call(f32[2,18,2,8,256]{4,3,2,1,0:T(8,128)S(1)} %get-tuple-element.4.g_ref, f32[2,2]{1,0:T(2,128)S(4)} %get-tuple-element.5.mon_ref), custom_call_target="tpu_custom_call" | custom-call | tf_op jit(solution)/shard_map/pallas_call | solution.py:684

commit v3 on v2

--- a/solution.py
+++ b/solution.py
@@ -244,7 +244,7 @@
     lane = lax.broadcasted_iota(jnp.int32, (depth, LANES), 1)
     column = lane % half
     strip = lane // half
-    flip = (me["ta"] + 1) // sizes["ta"]
+    flip = 1 - lax.rem(me["ta"], 2)
 
     def piece(h):
         return pl.ds(h * LANES if isinstance(h, int) else pl.multiple_of(h * LANES, LANES), LANES)
@@ -272,8 +272,8 @@
         return pltpu.make_async_remote_copy(
             src_ref=tsend.at[slot, way, :, :, piece(h)],
             dst_ref=trecv.at[slot, way, :, :, piece(h)],
-            send_sem=t_send_sem.at[slot, way, h],
-            recv_sem=t_recv_sem.at[slot, way, h],
+            send_sem=t_send_sem.at[slot % 2, way, h],
+            recv_sem=t_recv_sem.at[slot % 2, way, h],
             device_id=along_t(way),
             device_id_type=MESH,
         )
@@ -296,7 +296,7 @@
         first_copy(colour, way, h).start()
 
     def take_first(colour, way, h):
-        first_copy(colour, way, h).wait_recv()
+        first_copy(colour, way, h).wait()
         m = decode(get(erecv, (colour, way), h, 8))
         put(halo, (colour, way), h, m)
         return m
@@ -307,8 +307,8 @@
             pltpu.make_async_remote_copy(
                 src_ref=src.at[k, way, t],
                 dst_ref=dst.at[k, way, t],
-                send_sem=side_send_sem.at[k, 2 * number + way, t],
-                recv_sem=side_recv_sem.at[k, 2 * number + way, t],
+                send_sem=side_send_sem.at[k % 2, 2 * number + way, t],
+                recv_sem=side_recv_sem.at[k % 2, 2 * number + way, t],
                 device_id=peer(axis, 1 if way else -1),
                 device_id_type=MESH,
             )
@@ -460,7 +460,7 @@
 
         def take(way, h):
             def turn():
-                t_copy(k - 1, way, h).wait_recv()
+                t_copy(k - 1, way, h).wait()
                 q = get(trecv, (k - 1, way), h, 12)
                 m = get(cb, (way,), h, 18)
                 for number, (i, j) in enumerate(PAIRS):
@@ -496,7 +496,7 @@
             ahead = 1 - back
             t = ahead * last
             for copy in side(k, t):
-                copy.wait_recv()
+                copy.wait()
             for h in range(nh):
                 along_yz(t, h)
             for h in range(nh):
@@ -535,10 +535,17 @@
 
         lax.fori_loop(0, slices, slab, 0)
 
-    for way in range(2):
-        loads[way].wait()
-        for h in range(nh):
-            send_first(1, way, h)
+    def send_both(colour):
+        for order in range(2):
+            @pl.when(flip == 1 - order)
+            def _():
+                for way in (order, 1 - order):
+                    for h in range(nh):
+                        send_first(colour, way, h)
+
+    loads[0].wait()
+    loads[1].wait()
+    send_both(1)
     loads[2].wait()
     for t in range(slices):
         for h in range(nh):
@@ -546,10 +553,9 @@
         for copy in side(0, t):
             copy.start()
 
-    for way in range(2):
-        loads[3 + way].wait()
-        for h in range(nh):
-            send_first(0, way, h)
+    loads[3].wait()
+    loads[4].wait()
+    send_both(0)
 
     def iteration(n, _):
         half_sweep(n, 0)
@@ -575,6 +581,8 @@
         for k in range(sizes["gy"])
         if i or j or k
     ]
+
+    toward = 1 - 2 * (2 * me["ta"] // sizes["ta"])
 
     def to_other(i, j, k):
         return pltpu.make_async_remote_copy(
@@ -600,23 +608,13 @@
     for t in range(slices):
         for h in range(nh):
             turn_own(steps - 1, 1, t, t, h)
+    arrivals.wait_send()
     arrivals.wait_recv()
     sums = total([plane[number] for number in range(lines)])
     sites = slices * depth * row_len * sizes["ta"] * width
     for n in range(ITERS):
         mon_out[0, n] = 1.0 - sums[0, 2 * n] / (24.0 * sites)
         mon_out[1, n] = sums[0, 2 * n + 1] / float(sites)
-    arrivals.wait_send()
-    for h in range(nh):
-        for way in range(2):
-            for colour in range(2):
-                first_copy(colour, way, h).wait_send()
-            for k in range(steps - 1):
-                t_copy(k, way, h).wait_send()
-    for k in range(steps):
-        for t in range(slices):
-            for copy in side(k, t):
-                copy.wait_send()
 
 
 def shards(sizes, lattice_links, transform):
@@ -659,12 +657,12 @@
             pltpu.VMEM((ITERS, 2, depth, LANES), f32),
             pltpu.VMEM((lines, 1, LANES), f32),
             pltpu.SemaphoreType.DMA((7,)),
-            pltpu.SemaphoreType.DMA((steps - 1, 2, nh)),
-            pltpu.SemaphoreType.DMA((steps - 1, 2, nh)),
             pltpu.SemaphoreType.DMA((2, 2, nh)),
             pltpu.SemaphoreType.DMA((2, 2, nh)),
-            pltpu.SemaphoreType.DMA((steps, 4, slices)),
-            pltpu.SemaphoreType.DMA((steps, 4, slices)),
+            pltpu.SemaphoreType.DMA((2, 2, nh)),
+            pltpu.SemaphoreType.DMA((2, 2, nh)),
+            pltpu.SemaphoreType.DMA((2, 4, slices)),
+            pltpu.SemaphoreType.DMA((2, 4, slices)),
             pltpu.SemaphoreType.DMA,
             pltpu.SemaphoreType.DMA,
         ],

time: 35.4 us -> 34.5 us (0.975)
  Pallas kernels: 34.6 us -> 33.7 us
    pallas_call x1, Pallas kernels: 33.7 us -> 32.9 us  [shards(): pl.pallas_call(functools.partial(kernel, sizes), out_shape=(pltpu.VMEM(tr...]
where the time goes in v3:
time: 34.5 us; the launch traced here: 34.4 us
  Pallas kernels  33.7 us (98%)
  between operations  0.64 us (2%)
    pallas_call x1, Pallas kernels, shards(): pl.pallas_call(functools.partial(kernel, sizes), out_shape=(pltpu.VMEM(tr...  32.9 us
    pallas_call x1, Pallas kernels, shards(): pl.pallas_call(finish, out_shape=(jax.ShapeDtypeStruct(transform.shape, f...  0.84 us

profile of v3, /device:TPU:0, one launch (start us, length us, event | category | flops | bytes accessed | tf_op | source)
XLA Modules:
  0.0 34.4 jit_solution(4014093536337697222)
XLA Ops:
  0.6 32.9 %shard_map.41 = (f32[2,18,2,8,256]{4,3,2,1,0:T(8,128)S(1)}, f32[2,2]{1,0:T(2,128)S(4)}) custom-call(f32[2,4,18,2,8,256]{5,4,3,2,1,0:T(8,128)} %links_hbm.1, f32[2,18,2,8,256]{4,3,2,1,0:T(8,128)} %trans_hbm.1), custom_call_target="tpu_custom_call" | custom-call | tf_op jit(solution)/shard_map/pallas_call | solution.py:631
  33.5 0.8 %shard_map.42 = (f32[2,18,2,8,256]{4,3,2,1,0:T(8,128)}, f32[2,2]{1,0:T(2,128)}) custom-call(f32[2,18,2,8,256]{4,3,2,1,0:T(8,128)S(1)} %get-tuple-element.4.g_ref, f32[2,2]{1,0:T(2,128)S(4)} %get-tuple-element.5.mon_ref), custom_call_target="tpu_custom_call" | custom-call | tf_op jit(solution)/shard_map/pallas_call | solution.py:682

commit v4 on v3

--- a/solution.py
+++ b/solution.py
@@ -85,16 +85,46 @@
 
 
 def rotate(m, q, i, j):
-    q0, q1, q2, q3 = q
+    q0, q1, q2 = q[:3]
     out = list(m)
     for k in range(3):
         ur, ui = m[3 * i + k], m[9 + 3 * i + k]
         lr, li = m[3 * j + k], m[9 + 3 * j + k]
-        out[3 * i + k] = q0 * ur - q3 * ui + q2 * lr - q1 * li
-        out[9 + 3 * i + k] = q0 * ui + q3 * ur + q2 * li + q1 * lr
-        out[3 * j + k] = q0 * lr + q3 * li - q2 * ur - q1 * ui
-        out[9 + 3 * j + k] = q0 * li - q3 * lr - q2 * ui + q1 * ur
+        values = [
+            q0 * ur + q2 * lr - q1 * li,
+            q0 * ui + q2 * li + q1 * lr,
+            q0 * lr - q2 * ur - q1 * ui,
+            q0 * li - q2 * ui + q1 * ur,
+        ]
+        if len(q) == 4:
+            turned = [-ui, ur, li, -lr]
+            values = [v + q[3] * u for v, u in zip(values, turned)]
+        out[3 * i + k], out[9 + 3 * i + k] = values[:2]
+        out[3 * j + k], out[9 + 3 * j + k] = values[2:]
     return out
+
+
+PARTS = (slice(0, 3), slice(3, 7), slice(7, 11))
+
+
+def turn(m, q):
+    for part, (i, j) in zip(PARTS, PAIRS):
+        m = rotate(m, q[part], i, j)
+    return m
+
+
+def reduced(first, second, third):
+    r0, r1, r2, r3 = first
+    square = r0 * r0 + r3 * r3
+    small = square < FLOOR
+    inv = lax.rsqrt(jnp.where(small, 1.0, square))
+    phase = (jnp.where(small, 1.0, r0 * inv), jnp.where(small, 0.0, -r3 * inv))
+    back = (phase[0], -phase[1])
+    a2, a1 = cmul(phase, (r2, r1))
+    b0, b3 = cmul(back, (second[0], second[3]))
+    c0, c3 = cmul(phase, (third[0], third[3]))
+    c2, c1 = cmul(back, (third[2], third[1]))
+    return [square * inv, a1, a2, b0, second[1], second[2], b3, c0, c1, c2, c3]
 
 
 def third_row(m):
@@ -351,10 +381,7 @@
             zsend[k, 1, t, comp : comp + 1, piece(h)] = prod_z[comp][depth - 1 : depth]
 
     def turn_own(k, c, t, way, h):
-        q = get(tsend, (k, way), h, 12)
-        own = load(g, c, t, h)
-        for number, (i, j) in enumerate(PAIRS):
-            own = rotate(own, q[4 * number : 4 * number + 4], i, j)
+        own = turn(load(g, c, t, h), get(tsend, (k, way), h, 11))
         store(g, own, c, t, h)
         return own
 
@@ -398,10 +425,7 @@
                 )
 
             def turned_halo(way):
-                m = get(halo, (p, way), h, 18)
-                q = get(trecv, (k - 3, way), h, 12)
-                for number, (i, j) in enumerate(PAIRS):
-                    m = rotate(m, q[4 * number : 4 * number + 4], i, j)
+                m = turn(get(halo, (p, way), h, 18), get(trecv, (k - 3, way), h, 11))
                 put(halo, (p, way), h, m)
                 return m
 
@@ -459,23 +483,20 @@
             store(w, mul(load(g, c, t, h), acc), t, h)
 
         def take(way, h):
-            def turn():
+            def later():
                 t_copy(k - 1, way, h).wait()
-                q = get(trecv, (k - 1, way), h, 12)
-                m = get(cb, (way,), h, 18)
-                for number, (i, j) in enumerate(PAIRS):
-                    m = rotate(m, q[4 * number : 4 * number + 4], i, j)
+                m = turn(get(cb, (way,), h, 18), get(trecv, (k - 1, way), h, 11))
                 put(cb, (way,), h, m)
 
             if c == 1:
-                turn()
+                later()
                 return
 
             @pl.when(n == 0)
             def _():
                 put(cb, (way,), h, mul_adj(take_first(p, way, h), get(cb, (way,), h, 18)))
 
-            pl.when(n > 0)(turn)
+            pl.when(n > 0)(later)
 
         def monitor(a):
             func = a[0] + a[4] + a[8]
@@ -505,9 +526,9 @@
                 turns = []
                 for i, j in PAIRS:
                     q = rotation(a, i, j)
-                    turns.extend(q)
+                    turns.append(q)
                     a = rotate(a, q, i, j)
-                put(tsend, (k, ahead), h, turns)
+                put(tsend, (k, ahead), h, reduced(*turns))
 
                 if c == 0:
                     t_copy(k, ahead, h).start()
@@ -645,8 +666,8 @@
             pltpu.VMEM((2, 18, depth, row_len), f32),
             pltpu.VMEM(face, f32),
             pltpu.VMEM(face, f32),
-            pltpu.VMEM((steps, 2, 12, depth, row_len), f32),
-            pltpu.VMEM((steps, 2, 12, depth, row_len), f32),
+            pltpu.VMEM((steps, 2, 11, depth, row_len), f32),
+            pltpu.VMEM((steps, 2, 11, depth, row_len), f32),
             pltpu.VMEM((2, 2, 18, depth, row_len), f32),
             pltpu.VMEM((2, 2, 8, depth, row_len), f32),
             pltpu.VMEM((2, 2, 8, depth, row_len), f32),

time: 34.5 us -> 33.8 us (0.980)
  Pallas kernels: 33.7 us -> 33 us
    pallas_call x1, Pallas kernels: 32.9 us -> 32.1 us  [shards(): pl.pallas_call(functools.partial(kernel, sizes), out_shape=(pltpu.VMEM(tr...]
where the time goes in v4:
time: 33.8 us; the launch traced here: 33.6 us
  Pallas kernels  33 us (98%)
  between operations  0.64 us (2%)
    pallas_call x1, Pallas kernels, shards(): pl.pallas_call(functools.partial(kernel, sizes), out_shape=(pltpu.VMEM(tr...  32.1 us
    pallas_call x1, Pallas kernels, shards(): pl.pallas_call(finish, out_shape=(jax.ShapeDtypeStruct(transform.shape, f...  0.84 us

profile of v4, /device:TPU:0, one launch (start us, length us, event | category | flops | bytes accessed | tf_op | source)
XLA Modules:
  0.0 33.6 jit_solution(5222371729386220)
XLA Ops:
  0.6 32.1 %shard_map.41 = (f32[2,18,2,8,256]{4,3,2,1,0:T(8,128)S(1)}, f32[2,2]{1,0:T(2,128)S(4)}) custom-call(f32[2,4,18,2,8,256]{5,4,3,2,1,0:T(8,128)} %links_hbm.1, f32[2,18,2,8,256]{4,3,2,1,0:T(8,128)} %trans_hbm.1), custom_call_target="tpu_custom_call" | custom-call | tf_op jit(solution)/shard_map/pallas_call | solution.py:652
  32.8 0.8 %shard_map.42 = (f32[2,18,2,8,256]{4,3,2,1,0:T(8,128)}, f32[2,2]{1,0:T(2,128)}) custom-call(f32[2,18,2,8,256]{4,3,2,1,0:T(8,128)S(1)} %get-tuple-element.4.g_ref, f32[2,2]{1,0:T(2,128)S(4)} %get-tuple-element.5.mon_ref), custom_call_target="tpu_custom_call" | custom-call | tf_op jit(solution)/shard_map/pallas_call | solution.py:703

commit v5 on v4

--- a/solution.py
+++ b/solution.py
@@ -611,7 +611,7 @@
             dst_ref=plane.at[here],
             send_sem=red_send,
             recv_sem=red_recv,
-            device_id=peer("ta", i) | peer("gz", j) | peer("gy", k),
+            device_id=peer("ta", i * toward) | peer("gz", j) | peer("gy", k),
             device_id_type=MESH,
         )
 

time: 33.8 us -> 33.7 us (level)
  no operation moved by 1% of the time
where the time goes in v5:
time: 33.7 us; the launch traced here: 33.5 us
  Pallas kernels  32.9 us (98%)
  between operations  0.64 us (2%)
    pallas_call x1, Pallas kernels, shards(): pl.pallas_call(functools.partial(kernel, sizes), out_shape=(pltpu.VMEM(tr...  32.1 us
    pallas_call x1, Pallas kernels, shards(): pl.pallas_call(finish, out_shape=(jax.ShapeDtypeStruct(transform.shape, f...  0.84 us

profile of v5, /device:TPU:0, one launch (start us, length us, event | category | flops | bytes accessed | tf_op | source)
XLA Modules:
  0.0 33.5 jit_solution(2147030971206603522)
XLA Ops:
  0.6 32.1 %shard_map.41 = (f32[2,18,2,8,256]{4,3,2,1,0:T(8,128)S(1)}, f32[2,2]{1,0:T(2,128)S(4)}) custom-call(f32[2,4,18,2,8,256]{5,4,3,2,1,0:T(8,128)} %links_hbm.1, f32[2,18,2,8,256]{4,3,2,1,0:T(8,128)} %trans_hbm.1), custom_call_target="tpu_custom_call" | custom-call | tf_op jit(solution)/shard_map/pallas_call | solution.py:652
  32.7 0.8 %shard_map.42 = (f32[2,18,2,8,256]{4,3,2,1,0:T(8,128)}, f32[2,2]{1,0:T(2,128)}) custom-call(f32[2,18,2,8,256]{4,3,2,1,0:T(8,128)S(1)} %get-tuple-element.4.g_ref, f32[2,2]{1,0:T(2,128)S(4)} %get-tuple-element.5.mon_ref), custom_call_target="tpu_custom_call" | custom-call | tf_op jit(solution)/shard_map/pallas_call | solution.py:703
